TPU v7x, 32 devices: a whole 2x2x4 slice. The times are simulated.
32 devices in a mesh: grp: 2 (over y), tm: 4 (over z), chan: 2 (over x), sub: 2 (over core).
Axes of the slice: x: 2, y: 2, z: 4, core: 2. Of those that a mesh axis runs over, the one named last changes fastest.
Arguments:
- signal: float32 [64, 131072], P(('grp', 'chan', 'sub'), 'tm'), parts along dimension 0, may hold values from -24 to 24
- gap_mask: int32 [64, 8], P(('grp', 'chan', 'sub'), 'tm'), parts along dimension 0, may hold values from 0 to 1, as said below
- assignment: int32 [64], P(('grp', 'chan', 'sub')), parts along dimension 0, may hold values from 0 to 7, as said below
Outputs:
- peak_hold: float32 [64, 16384], P(('grp', 'chan', 'sub'), 'tm'), parts along dimension 0
- log_mean: float32 [64, 16384], P(('grp', 'chan', 'sub'), 'tm'), parts along dimension 0
- block_mean: float32 [16, 16384], P('grp', 'tm'), parts along dimension 0
There are 2 independent parts, one for each index of `grp`. A program takes and returns all parts, laid end to end along the dimension named above; each array names one. Nothing has to cross between parts.
Inputs may be any that keep to these rules, and one draw needn't show every extreme that they name: `gap_mask`: every channel keeps at least one of its 8 segments. `assignment`: every block holds at least one channel.
All inputs are finite; a program needn't handle non-finite values.
Results may differ from a plain program's by a relative error of at most 0.000086.
Values sent between devices are 32-bit elements; how exact they have to be, the bound alone decides.
A program may use at most 128 MiB of HBM per device.

v0:
```python
import math
import jax
import jax.numpy as jnp
from jax import lax
from jax.sharding import PartitionSpec as P

LA = 256
LB = 128
BLOCKS = 8


def from_behind(x, axis, by):
    count = lax.axis_size(axis)
    pairs = [(i, i + by) for i in range(count) if 0 <= i + by < count]
    return lax.ppermute(x, axis, pairs)


def rotations(height, columns, modulus):
    products = (
        jnp.arange(height, dtype=jnp.int32)[:, None]
        * jnp.arange(columns, dtype=jnp.int32)[None, :]
        % modulus
    )
    angles = products.astype(jnp.float32) * (2.0 * math.pi / modulus)
    return (jnp.cos(angles), -jnp.sin(angles))


def on_device(signal, gap_mask, assignment):
    channels, local_time = signal.shape
    seg_local = gap_mask.shape[1]
    half = local_time // seg_local
    seg_length = LA * LB
    highest = lax.Precision.HIGHEST
    borrowed = from_behind(signal[:, :half], "tm", -1)
    extended = jnp.concatenate([signal, borrowed], axis=1)
    hop_rows = extended.reshape(channels, seg_local + 1, half)
    section_one = rotations(LB, LB, LB)
    twiddle = rotations(LB, LA, seg_length)
    section_two = rotations(LA, LA // 2, LA)
    samples = jnp.arange(seg_length, dtype=jnp.float32)
    window = (0.5 - 0.5 * jnp.cos(samples * (2.0 * math.pi / seg_length))).reshape(LB, LA)
    norm_scale = 1.0 / (0.375 * seg_length)

    def one_channel(inputs):
        rows_here, keep_flags = inputs
        segments = jnp.concatenate([rows_here[:-1], rows_here[1:]], axis=-1)
        frames = segments.reshape(seg_local, LB, LA) * window
        real_one = jnp.einsum("kb,sba->ska", section_one[0], frames, precision=highest)
        imag_one = jnp.einsum("kb,sba->ska", section_one[1], frames, precision=highest)
        real_mid = real_one * twiddle[0] - imag_one * twiddle[1]
        imag_mid = real_one * twiddle[1] + imag_one * twiddle[0]
        real_two = jnp.einsum(
            "ska,aj->skj", real_mid, section_two[0], precision=highest
        ) - jnp.einsum("ska,aj->skj", imag_mid, section_two[1], precision=highest)
        imag_two = jnp.einsum(
            "ska,aj->skj", real_mid, section_two[1], precision=highest
        ) + jnp.einsum("ska,aj->skj", imag_mid, section_two[0], precision=highest)
        powers = (real_two * real_two + imag_two * imag_two) * norm_scale
        powers = jnp.swapaxes(powers, 1, 2).reshape(seg_local, -1)
        weights = keep_flags.astype(jnp.float32)
        peak_local = jnp.max(powers * weights[:, None], axis=0)
        log_terms = jnp.sum(weights[:, None] * jnp.log(0.25 + powers), axis=0)
        return (peak_local, log_terms)

    peak_local, log_terms = lax.map(one_channel, (hop_rows, gap_mask))
    kept_local = jnp.sum(gap_mask.astype(jnp.float32), axis=1)
    time_devices = lax.axis_size("tm")
    bin_width = peak_local.shape[1] // time_devices
    count_terms = jnp.broadcast_to(kept_local[:, None], (channels, time_devices))
    peak_all = lax.pmax(peak_local, "tm")
    peak_hold = lax.dynamic_slice_in_dim(peak_all, lax.axis_index("tm") * bin_width, bin_width, 1)
    log_sum, kept_total = (
        lax.psum_scatter(log_terms, "tm", scatter_dimension=1, tiled=True),
        lax.psum_scatter(count_terms, "tm", scatter_dimension=1, tiled=True),
    )
    log_mean = log_sum / kept_total
    onehot = (assignment[None, :] == jnp.arange(BLOCKS, dtype=jnp.int32)[:, None]).astype(
        jnp.float32
    )
    block_part = jnp.dot(onehot, log_mean, precision=highest)
    block_total, block_counts = lax.psum((block_part, jnp.sum(onehot, axis=1)), ("chan", "sub"))
    block_mean = block_total / block_counts[:, None]
    return (peak_hold, log_mean, block_mean)


def solution(mesh):
    in_specs = (
        P(("grp", "chan", "sub"), "tm"),
        P(("grp", "chan", "sub"), "tm"),
        P(("grp", "chan", "sub")),
    )
    out_specs = (P(("grp", "chan", "sub"), "tm"), P(("grp", "chan", "sub"), "tm"), P("grp", "tm"))
    return jax.shard_map(
        on_device, mesh=mesh, in_specs=in_specs, out_specs=out_specs, check_vma=False
    )
```

profile of v0, /device:TPU:0, one launch (start us, length us, event | category | flops | bytes accessed | tf_op | source)
XLA Modules:
  0.0 217.9 jit_solution(8996956551035906242)
XLA Ops:
  7.2 1.2 slice.11
  8.4 1.3 collective-permute-start
  10.5 14.9 %collective-permute-done = f32[8,16384]{1,0:T(8,128)} collective-permute-done((f32[8,16384]{1,0:T(8,128)S(1)}, f32[8,16384]{1,0:T(8,128)}, u32[]{:S(2)}, u32[]{:S(2)}) %collective-permute-start) | collective-permute-done | bytes 524320 | tf_op jit(solution)/shard_map/ppermute | solution.py:15
  26.5 2.5 %reshape.43 = f32[8,3,16384]{2,1,0:T(4,128)} reshape(f32[8,49152]{1,0:T(8,128)S(1)} %pad_maximum_fusion) | data formatting | bytes 3145728 | tf_op jit(solution)/shard_map/reshape | solution.py:36
  29.0 84.5 %while.14 = (s32[]{:T(128)}, f32[8,16384]{1,0:T(8,128)S(1)}, f32[8,16384]{1,0:T(8,128)}, f32[8,3,16384]{2,1,0:T(4,128)}, s32[8,2]{1,0:T(8,128)S(1)}, /*index=5*/s32[]{:T(128)}, s32[]{:T(128)}, s32[]{}) while((s32[]{:T(128)}, f32[8,16384]{1,0:T(8,128)S(1)}, f32[8,16384]{1,0:T(8,128)}, f32[8,3,16384]{2,1,0:T(4,128)}, ...), condition=%wide.region_3.4_spmd.clone.clone, body=%wide.region_0.3_spmd.clone.clone.sunk | while | flops 608321536 | bytes 8388765 | solution.py:65
  29.0 1.2 constant_dynamic-slice_fusion.5
  37.1 1.9 dynamic_update_slice.14
  39.6 1.1 constant_dynamic-slice_fusion.5
  47.6 1.9 dynamic_update_slice.14
  50.2 1.1 constant_dynamic-slice_fusion.5
  58.2 1.9 dynamic_update_slice.14
  60.7 1.1 constant_dynamic-slice_fusion.5
  68.7 1.9 dynamic_update_slice.14
  79.3 1.9 dynamic_update_slice.14
  89.9 1.9 dynamic_update_slice.14
  100.4 1.9 dynamic_update_slice.14
  111.0 1.9 dynamic_update_slice.14
  113.7 5.9 %psum.15 = f32[8]{0:T(128)S(1)} all-reduce(f32[8]{0:T(128)S(1)} %convert_reduce_fusion), channel_id=1, replica_groups=mesh['grp'=2,'tm'=4,'chan'=2,'sub'=2] {'chan','sub'}, use_global_device_ids=true, to_apply=%region_10.11 | all-reduce | flops 8 | bytes 64 | tf_op jit(solution)/shard_map/psum | solution.py:81
  120.2 10.0 %all-reduce = f32[8,4]{0,1:T(4,128)S(1)} all-reduce(f32[8,4]{0,1:T(4,128)S(1)} %broadcast_in_dim.8), channel_id=3, replica_groups=mesh['grp'=2,'tm'=4,'chan'=2,'sub'=2] {'tm'}, use_global_device_ids=true, to_apply=%region_7.8.clone | all-reduce | flops 32 | bytes 256
  131.0 5.0 %reduce-scatter.2.cloned.1.call-done = f32[8,4096]{1,0:T(8,128)} async-done(((f32[8,16384]{1,0:T(8,128)}), f32[8,4096]{1,0:T(8,128)}) %reduce-scatter.2.cloned.1.call-update) | async-done | bytes 131088 | tf_op jit(solution)/shard_map/reduce_scatter | solution.py:73
  137.9 37.3 %all-reduce.4.cloned.1.call-done = f32[8,16384]{1,0:T(8,128)} async-done(((f32[8,16384]{1,0:T(8,128)}), f32[8,16384]{1,0:T(8,128)}) %all-reduce.4.cloned.1.call-update) | async-done | bytes 524304 | tf_op jit(solution)/shard_map/pmax | solution.py:70
  175.2 1.6 constant_dynamic-slice_fusion.3
  176.8 32.9 %all-reduce.6.cloned.1.call-done = f32[8,4096]{1,0:T(8,128)} async-done(((f32[8,4096]{1,0:T(8,128)}), f32[8,4096]{1,0:T(8,128)}) %all-reduce.6.cloned.1.call-update) | async-done | bytes 131088 | tf_op jit(solution)/shard_map/psum | solution.py:81
  209.7 1.6 broadcast_divide_fusion
  (177 shorter events, 68.5 us)
Async XLA Ops:
  7.2 18.2 %copy-start = (f32[8,32768]{1,0:T(8,128)S(1)}, f32[8,32768]{1,0:T(8,128)}, u32[]{:S(2)}) copy-start(f32[8,32768]{1,0:T(8,128)} %param.5) | copy-start | bytes 3145732
  7.2 128.9 %reduce-scatter.2.cloned.1.call-start = ((), (), s32[]{:S(2)}) async-start(), calls=%async_computation.2 | async-start | bytes 655360 | tf_op jit(solution)/shard_map/reduce_scatter | solution.py:73
  8.4 17.0 %collective-permute-start = (f32[8,16384]{1,0:T(8,128)S(1)}, f32[8,16384]{1,0:T(8,128)}, u32[]{:S(2)}, u32[]{:S(2)}) collective-permute-start(f32[8,16384]{1,0:T(8,128)S(1)} %slice.11), channel_id=1, source_target_pairs={{4,0},{8,4},{12,8},{5,1},{9,5},{13,9},{6,2},{10,6},{14,10},{7,3},{... | collective-permute-start | bytes 1572872 | tf_op jit(solution)/shard_map/ppermute | solution.py:15
  29.0 84.6 %copy-start.4 = (s32[8]{0:T(128)S(1)}, s32[8]{0:T(128)}, u32[]{:S(2)}) copy-start(s32[8]{0:T(128)} %param.7) | copy-start | bytes 100
  29.0 90.6 %copy-start.5 = (u32[32]{0:T(128)S(1)}, u32[32]{0:T(128)}, u32[]{:S(2)}) copy-start(u32[32]{0:T(128)} %constant.88) | copy-start | bytes 388
  29.0 91.2 %copy-start.3 = (s32[8,2]{0,1:T(2,128)S(1)}, s32[8,2]{0,1:T(2,128)}, u32[]{:S(2)}) copy-start(s32[8,2]{0,1:T(2,128)} %param.6) | copy-start | bytes 196
  113.5 17.4 %copy-start.1 = (f32[8,16384]{1,0:T(8,128)}, f32[8,16384]{1,0:T(8,128)S(1)}, u32[]{:S(2)}) copy-start(f32[8,16384]{1,0:T(8,128)S(1)} %get-tuple-element.78) | copy-start | bytes 1572868
  113.6 61.7 %all-reduce.4.cloned.1.call-start = ((), (), s32[]{:S(2)}) async-start(), calls=%async_computation.1 | async-start | bytes 1048576 | tf_op jit(solution)/shard_map/pmax | solution.py:70
  131.0 78.8 %all-reduce.6.cloned.1.call-start = ((), (), s32[]{:S(2)}) async-start(), calls=%async_computation.3 | async-start | bytes 262144 | tf_op jit(solution)/shard_map/psum | solution.py:81
  137.0 74.4 %copy-start.2 = (f32[8,4096]{1,0:T(8,128)}, f32[8,4096]{1,0:T(8,128)S(1)}, u32[]{:S(2)}) copy-start(f32[8,4096]{1,0:T(8,128)S(1)} %broadcast_divide_fusion.1) | copy-start | bytes 393220
Sparse Core Ops, SparseCore 0:
  113.7 22.3 reduce-scatter.1
  138.4 36.8 all-reduce.3
  178.1 31.5 all-reduce.5
where the time goes:
time: 219 us; the launch traced here: 218 us
  waiting for transfers between devices  90.2 us (41%)
  matrix products  42.8 us (20%)
  local copies, waits for them, and re-layouts  40.5 us (18%)
  blocking collectives  15.9 us (7%)
  between operations  13.8 us (6%)
  other arithmetic  12 us (5%)
    pmax x1, waiting for transfers between devices, on_device(): peak_all = lax.pmax(peak_local, 'tm')  37.3 us
    psum x1, waiting for transfers between devices, on_device(): lax.psum((block_part, jnp.sum(onehot, axis=1)), ('chan', 'sub'))  32.9 us
    dynamic_update_slice x16, local copies, waits for them, and re-layouts, on_device(): peak_local, log_terms = lax.map(one_channel, (hop_rows, gap_mask))  19.5 us
    ppermute x1, waiting for transfers between devices, from_behind(): return lax.ppermute(x, axis, pairs)  14.9 us
    unnamed x1, blocking collectives  10 us
    slice x8, local copies, waits for them, and re-layouts, one_channel(): segments = jnp.concatenate([rows_here[:-1], rows_here[1:]], axis=-1)  9.22 us
    dot_general x8, matrix products, one_channel(): jnp.einsum('ska,aj->skj', imag_mid, section_two[0], precision=highest)  8.05 us
    dot_general x8, matrix products, one_channel(): jnp.einsum('ska,aj->skj', real_mid, section_two[0], precision=highest)  7.94 us
  transfers between devices with their start and end apart: 4, of which 4 were waited for; matrix products, arithmetic and copies ran while one was open for 3% of the time, Pallas kernels for 0%

commit v1 on v0

--- a/solution.py
+++ b/solution.py
@@ -78,7 +78,11 @@
         jnp.float32
     )
     block_part = jnp.dot(onehot, log_mean, precision=highest)
-    block_total, block_counts = lax.psum((block_part, jnp.sum(onehot, axis=1)), ("chan", "sub"))
+
+    def change_limits(mine_x):
+        return lax.psum(lax.psum(mine_x, axis_name="sub"), axis_name="chan")
+
+    block_total, block_counts = change_limits((block_part, jnp.sum(onehot, axis=1)))
     block_mean = block_total / block_counts[:, None]
     return (peak_hold, log_mean, block_mean)
 

time: 219 us -> 229 us (1.046)
  waiting for transfers between devices: 90.2 us -> 99.4 us
    reduce_scatter x1, waiting for transfers between devices: 5.01 us -> 10.8 us  [on_device(): lax.psum_scatter(log_terms, 'tm', scatter_dimension=1, tiled=True)]
    pmax x1, waiting for transfers between devices: 37.3 us -> 42.1 us  [on_device(): peak_all = lax.pmax(peak_local, 'tm')]
    psum x1 -> x2, waiting for transfers between devices: 32.9 us -> 30.9 us  [change_limits(): return lax.psum(lax.psum(mine_x, axis_name='sub'), axis_name='chan')]
    psum x1 -> x2, blocking collectives: 5.9 us -> 7.37 us  [change_limits(): return lax.psum(lax.psum(mine_x, axis_name='sub'), axis_name='chan')]
  transfers between devices with their start and end apart: 4 -> 5, of which waited for: 4 -> 5; matrix products, arithmetic and copies ran while one was open for 3% -> 2% of each run, Pallas kernels for 0% -> 0%
where the time goes in v1:
time: 229 us
  waiting for transfers between devices  99.4 us (43%)
  matrix products  42.8 us (19%)
  local copies, waits for them, and re-layouts  40.5 us (18%)
  blocking collectives  17.5 us (8%)
  between operations  13.9 us (6%)
  other arithmetic  12 us (5%)
    pmax x1, waiting for transfers between devices, on_device(): peak_all = lax.pmax(peak_local, 'tm')  42.1 us
    psum x2, waiting for transfers between devices, change_limits(): return lax.psum(lax.psum(mine_x, axis_name='sub'), axis_name='chan')  30.9 us
    dynamic_update_slice x16, local copies, waits for them, and re-layouts, on_device(): peak_local, log_terms = lax.map(one_channel, (hop_rows, gap_mask))  19.5 us
    ppermute x1, waiting for transfers between devices, from_behind(): return lax.ppermute(x, axis, pairs)  14.9 us
    reduce_scatter x1, waiting for transfers between devices, on_device(): lax.psum_scatter(log_terms, 'tm', scatter_dimension=1, tiled=True)  10.8 us
    unnamed x1, blocking collectives  10.2 us
    slice x8, local copies, waits for them, and re-layouts, one_channel(): segments = jnp.concatenate([rows_here[:-1], rows_here[1:]], axis=-1)  9.22 us
    dot_general x8, matrix products, one_channel(): jnp.einsum('ska,aj->skj', imag_mid, section_two[0], precision=highest)  8.05 us
  transfers between devices with their start and end apart: 5, of which 5 were waited for; matrix products, arithmetic and copies ran while one was open for 2% of the time, Pallas kernels for 0%

profile of v1, /device:TPU:0, one launch (start us, length us, event | category | flops | bytes accessed | tf_op | source)
XLA Modules:
  0.0 228.8 jit_solution(11907317303194092478)
XLA Ops:
  7.2 1.2 slice.11
  8.4 1.3 collective-permute-start
  10.5 14.9 %collective-permute-done = f32[8,16384]{1,0:T(8,128)} collective-permute-done((f32[8,16384]{1,0:T(8,128)S(1)}, f32[8,16384]{1,0:T(8,128)}, u32[]{:S(2)}, u32[]{:S(2)}) %collective-permute-start) | collective-permute-done | bytes 524320 | tf_op jit(solution)/shard_map/ppermute | solution.py:15
  26.5 2.5 %reshape.43 = f32[8,3,16384]{2,1,0:T(4,128)} reshape(f32[8,49152]{1,0:T(8,128)S(1)} %pad_maximum_fusion) | data formatting | bytes 3145728 | tf_op jit(solution)/shard_map/reshape | solution.py:36
  29.0 84.5 %while.14 = (s32[]{:T(128)}, f32[8,16384]{1,0:T(8,128)S(1)}, f32[8,16384]{1,0:T(8,128)}, f32[8,3,16384]{2,1,0:T(4,128)}, s32[8,2]{1,0:T(8,128)S(1)}, /*index=5*/s32[]{:T(128)}, s32[]{:T(128)}, s32[]{}) while((s32[]{:T(128)}, f32[8,16384]{1,0:T(8,128)S(1)}, f32[8,16384]{1,0:T(8,128)}, f32[8,3,16384]{2,1,0:T(4,128)}, ...), condition=%wide.region_3.4_spmd.clone.clone, body=%wide.region_0.3_spmd.clone.clone.sunk | while | flops 608321536 | bytes 8388765 | solution.py:65
  29.0 1.2 constant_dynamic-slice_fusion.5
  37.1 1.9 dynamic_update_slice.14
  39.6 1.1 constant_dynamic-slice_fusion.5
  47.6 1.9 dynamic_update_slice.14
  58.2 1.9 dynamic_update_slice.14
  68.7 1.9 dynamic_update_slice.14
  79.3 1.9 dynamic_update_slice.14
  89.9 1.9 dynamic_update_slice.14
  100.4 1.9 dynamic_update_slice.14
  111.0 1.9 dynamic_update_slice.14
  114.2 10.2 %all-reduce = f32[8,4]{0,1:T(4,128)S(1)} all-reduce(f32[8,4]{0,1:T(4,128)S(1)} %broadcast_in_dim.8), channel_id=3, replica_groups=mesh['grp'=2,'tm'=4,'chan'=2,'sub'=2] {'tm'}, use_global_device_ids=true, to_apply=%region_7.8.clone | all-reduce | flops 32 | bytes 256
  125.1 10.8 %reduce-scatter.2.cloned.1.call-done = f32[8,4096]{1,0:T(8,128)} async-done(((f32[8,16384]{1,0:T(8,128)}), f32[8,4096]{1,0:T(8,128)}) %reduce-scatter.2.cloned.1.call-update) | async-done | bytes 131088 | tf_op jit(solution)/shard_map/reduce_scatter | solution.py:73
  138.7 2.5 %psum.30 = f32[8]{0:T(128)S(1)} all-reduce(f32[8]{0:T(128)S(1)} %convert_reduce_fusion), channel_id=1, replica_groups=mesh['grp'=2,'tm'=4,'chan'=2,'sub'=2] {'sub'}, use_global_device_ids=true, to_apply=%region_11.12 | all-reduce | flops 8 | bytes 64 | tf_op jit(solution)/shard_map/psum | solution.py:83
  141.2 4.9 %psum.31 = f32[8]{0:T(128)S(1)} all-reduce(f32[8]{0:T(128)S(1)} %psum.30), channel_id=1, replica_groups=mesh['grp'=2,'tm'=4,'chan'=2,'sub'=2] {'chan'}, use_global_device_ids=true, to_apply=%region_12.13 | all-reduce | flops 8 | bytes 64 | tf_op jit(solution)/shard_map/psum | solution.py:83
  146.1 8.9 %all-reduce.7.cloned.1.call-done = f32[8,4096]{1,0:T(8,128)} async-done(((f32[8,4096]{1,0:T(8,128)}), f32[8,4096]{1,0:T(8,128)}) %all-reduce.7.cloned.1.call-update) | async-done | bytes 131088 | tf_op jit(solution)/shard_map/psum | solution.py:83
  155.0 42.1 %all-reduce.5.cloned.1.call-done = f32[8,16384]{1,0:T(8,128)} async-done(((f32[8,16384]{1,0:T(8,128)}), f32[8,16384]{1,0:T(8,128)}) %all-reduce.5.cloned.1.call-update) | async-done | bytes 524304 | tf_op jit(solution)/shard_map/pmax | solution.py:70
  197.1 1.6 constant_dynamic-slice_fusion.3
  198.7 21.9 %all-reduce.9.cloned.1.call-done = f32[8,4096]{1,0:T(8,128)} async-done(((f32[8,4096]{1,0:T(8,128)}), f32[8,4096]{1,0:T(8,128)}) %all-reduce.9.cloned.1.call-update) | async-done | bytes 131088 | tf_op jit(solution)/shard_map/psum | solution.py:83
  220.6 1.6 broadcast_divide_fusion
  (181 shorter events, 71.5 us)
Async XLA Ops:
  7.2 18.2 %copy-start = (f32[8,32768]{1,0:T(8,128)S(1)}, f32[8,32768]{1,0:T(8,128)}, u32[]{:S(2)}) copy-start(f32[8,32768]{1,0:T(8,128)} %param.5) | copy-start | bytes 3145732
  7.2 128.7 %reduce-scatter.2.cloned.1.call-start = ((), (), s32[]{:S(2)}) async-start(), calls=%async_computation.2 | async-start | bytes 655360 | tf_op jit(solution)/shard_map/reduce_scatter | solution.py:73
  8.4 17.0 %collective-permute-start = (f32[8,16384]{1,0:T(8,128)S(1)}, f32[8,16384]{1,0:T(8,128)}, u32[]{:S(2)}, u32[]{:S(2)}) collective-permute-start(f32[8,16384]{1,0:T(8,128)S(1)} %slice.11), channel_id=1, source_target_pairs={{4,0},{8,4},{12,8},{5,1},{9,5},{13,9},{6,2},{10,6},{14,10},{7,3},{... | collective-permute-start | bytes 1572872 | tf_op jit(solution)/shard_map/ppermute | solution.py:15
  29.0 84.6 %copy-start.5 = (u32[32]{0:T(128)S(1)}, u32[32]{0:T(128)}, u32[]{:S(2)}) copy-start(u32[32]{0:T(128)} %constant.88) | copy-start | bytes 388
  29.0 85.2 %copy-start.3 = (s32[8,2]{0,1:T(2,128)S(1)}, s32[8,2]{0,1:T(2,128)}, u32[]{:S(2)}) copy-start(s32[8,2]{0,1:T(2,128)} %param.6) | copy-start | bytes 196
  29.0 107.9 %copy-start.4 = (s32[8]{0:T(128)S(1)}, s32[8]{0:T(128)}, u32[]{:S(2)}) copy-start(s32[8]{0:T(128)} %param.7) | copy-start | bytes 100
  113.5 24.3 %copy-start.1 = (f32[8,16384]{1,0:T(8,128)}, f32[8,16384]{1,0:T(8,128)S(1)}, u32[]{:S(2)}) copy-start(f32[8,16384]{1,0:T(8,128)S(1)} %get-tuple-element.78) | copy-start | bytes 1572868
  113.6 41.4 %all-reduce.7.cloned.1.call-start = ((), (), s32[]{:S(2)}) async-start(), calls=%async_computation.3 | async-start | bytes 262144 | tf_op jit(solution)/shard_map/psum | solution.py:83
  136.9 85.3 %copy-start.2 = (f32[8,4096]{1,0:T(8,128)}, f32[8,4096]{1,0:T(8,128)S(1)}, u32[]{:S(2)}) copy-start(f32[8,4096]{1,0:T(8,128)S(1)} %broadcast_divide_fusion.1) | copy-start | bytes 393220
  137.8 59.3 %all-reduce.5.cloned.1.call-start = ((), (), s32[]{:S(2)}) async-start(), calls=%async_computation.1 | async-start | bytes 1048576 | tf_op jit(solution)/shard_map/pmax | solution.py:70
  138.5 82.1 %all-reduce.9.cloned.1.call-start = ((), (), s32[]{:S(2)}) async-start(), calls=%async_computation.4 | async-start | bytes 262144 | tf_op jit(solution)/shard_map/psum | solution.py:83
Sparse Core Ops, SparseCore 0:
  113.7 22.1 reduce-scatter.1
  138.8 16.1 all-reduce.6
  157.3 39.7 all-reduce.4
  199.2 21.3 all-reduce.8
